TPU v7x, 32 devices: a whole 2x2x4 slice. The times are simulated.
32 devices in a mesh: freq: 4 (over y, x), space: 8 (over z, core).
Axes of the slice: x: 2, y: 2, z: 4, core: 2. Of those that a mesh axis runs over, the one named last changes fastest.
Arguments:
- spectra: bfloat16 [64, 24576, 256], P('freq', 'space'), may hold values from -48 to 48, as said below
- weight: float32 [24576], P('space'), may hold values from 0.25 to 4
- partner: int32 [64], P('freq'), may hold values from 0 to 15
- counts: int32 [64], P('freq'), may hold values from 1 to 8
Outputs:
- modes: bfloat16 [64, 16, 24576], P('freq', None, 'space')
- energy: float32 [64, 8], P('freq')
- coherence: float32 [64, 2, 8, 8], P('freq')
Inputs may be any that keep to these rules, and one draw needn't show every extreme that they name: spectra are finite Fourier coefficients.
All inputs are finite; a program needn't handle non-finite values.
Results may differ from a plain program's by a relative error of at most 0.0045.
Values may be sent and summed in bfloat16 or wider, within the bound.
A program may use at most 128 MiB of HBM per device.

v0:
```python
import jax
import jax.numpy as jnp
from jax import lax
from jax.sharding import PartitionSpec as P

KMAX = 8
ITERS = 4


def from_partner(block, axis, apart):
    count = lax.axis_size(axis)
    route = []
    for low in range(count):
        high = low | 1 << apart
        if high != low and high < count:
            route += [(low, high), (high, low)]
    return lax.ppermute(block, axis, route)


def embed(gram_re, gram_im):
    top = jnp.concatenate([gram_re, -gram_im], axis=2)
    bottom = jnp.concatenate([gram_im, gram_re], axis=2)
    return jnp.concatenate([top, bottom], axis=1)


def apply_operator(operator, basis):
    return jnp.einsum("fkc,fdc->fkd", basis, operator, precision=lax.Precision.HIGHEST)


def orthonormal(vectors, half):
    done = []
    for index in range(vectors.shape[1]):
        vector = vectors[:, index, :]
        for earlier in done:
            early_re, early_im = (earlier[:, :half], earlier[:, half:])
            vec_re, vec_im = (vector[:, :half], vector[:, half:])
            proj_re = jnp.sum(early_re * vec_re + early_im * vec_im, axis=1, keepdims=True)
            proj_im = jnp.sum(early_re * vec_im - early_im * vec_re, axis=1, keepdims=True)
            new_re = vec_re - proj_re * early_re + proj_im * early_im
            new_im = vec_im - proj_re * early_im - proj_im * early_re
            vector = jnp.concatenate([new_re, new_im], axis=1)
        length = jnp.sqrt(jnp.sum(vector * vector, axis=1, keepdims=True) + 1e-06)
        done.append(vector / length)
    return jnp.stack(done, axis=1)


def solve(gram_re, gram_im):
    half = gram_re.shape[1]
    operator = embed(gram_re, gram_im)
    basis = jnp.broadcast_to(
        jnp.eye(KMAX, 2 * half, dtype=jnp.float32), (gram_re.shape[0], KMAX, 2 * half)
    )
    for sweep in range(ITERS):
        basis = orthonormal(apply_operator(operator, basis), half)
    image = apply_operator(operator, basis)
    energy = jnp.sum(basis * image, axis=2)
    return (basis, energy)


def combine(moments, half, total):
    gram_re = (moments[:, :half, :half] + moments[:, half:, half:]) / total
    gram_im = (moments[:, :half, half:] - moments[:, half:, :half]) / total
    return (gram_re, gram_im)


def coefficients(basis, energy, counts):
    half = basis.shape[2] // 2
    ranks = jnp.arange(KMAX, dtype=jnp.int32)[None, :]
    scale = jnp.where(ranks < counts[:, None], 1.0 / jnp.sqrt(energy + 1e-06), 0.0)[:, :, None]
    part_re, part_im = (basis[:, :, :half], basis[:, :, half:])
    upper = jnp.concatenate([part_re, -part_im], axis=2) * scale
    lower = jnp.concatenate([part_im, part_re], axis=2) * scale
    return jnp.concatenate([upper, lower], axis=1).astype(jnp.bfloat16)


def cross_terms(own_modes, other_modes, point_weight, total):
    phi = own_modes.astype(jnp.float32)
    psi = other_modes.astype(jnp.float32)
    wphi = phi * point_weight[None, None, :]
    highest = lax.Precision.HIGHEST

    def inner(left, right):
        return jnp.einsum("fkp,flp->fkl", left, right, precision=highest)

    real_part = inner(wphi[:, :KMAX], psi[:, :KMAX]) + inner(wphi[:, KMAX:], psi[:, KMAX:])
    imag_part = inner(wphi[:, :KMAX], psi[:, KMAX:]) - inner(wphi[:, KMAX:], psi[:, :KMAX])
    return jnp.stack([real_part, imag_part], axis=1) / total


def on_device(spectra, weight, partner, counts):
    groups = spectra.shape[0]
    half = spectra.shape[2] // 2
    total = spectra.shape[1] * lax.axis_size("space")
    weighted = (weight[None, :, None] * spectra).astype(jnp.bfloat16)
    moments = lax.dot_general(
        spectra, weighted, (((1,), (1,)), ((0,), (0,))), preferred_element_type=jnp.float32
    )
    summed = lax.psum(moments, "space")
    gram_re, gram_im = combine(summed, half, total)
    basis, energy = solve(gram_re, gram_im)
    coefficient = coefficients(basis, energy, counts)
    modes = jnp.einsum(
        "fkc,fpc->fkp", coefficient, spectra, preferred_element_type=jnp.float32
    ).astype(jnp.bfloat16)
    levels = lax.axis_size("freq").bit_length() - 1
    mirrored = modes
    for bit in range(levels):
        mirrored = from_partner(mirrored, "freq", bit)
    match = (partner[:, None] == jnp.arange(groups, dtype=jnp.int32)[None, :]).astype(jnp.bfloat16)
    chosen = jnp.einsum("fg,gkp->fkp", match, mirrored, preferred_element_type=jnp.float32).astype(
        jnp.bfloat16
    )
    local = cross_terms(modes, chosen, weight, total)
    coherence = lax.psum(local, "space")
    return (modes, energy, coherence)


def solution(mesh):
    in_specs = (P("freq", "space", None), P("space"), P("freq"), P("freq"))
    out_specs = (P("freq", None, "space"), P("freq", None), P("freq", None, None, None))
    return jax.shard_map(
        on_device, mesh=mesh, in_specs=in_specs, out_specs=out_specs, check_vma=False
    )
```

profile of v0, /device:TPU:0, one launch (start us, length us, event | category | flops | bytes accessed | tf_op | source)
XLA Modules:
  0.0 290.2 jit_solution(2149110146235932898)
XLA Ops:
  7.2 20.7 %fusion.2 = f32[16,256,256]{1,2,0:T(8,128)} fusion(bf16[16,3072,256]{2,1,0:T(8,128)(2,1)} %param.4, f32[3072]{0:T(1024)} %param.5), kind=kOutput, calls=%fused_computation.7 | convolution fusion | flops 6480199680 | bytes 29372416 | tf_op jit(solution)/shard_map/dot_general | solution.py:95
  27.9 99.3 %all-reduce.2.cloned.1.call-done = f32[16,256,256]{1,2,0:T(8,128)} async-done(((f32[16,256,256]{1,2,0:T(8,128)}), f32[16,256,256]{1,2,0:T(8,128)}) %all-reduce.2.cloned.1.call-update) | async-done | bytes 4194320 | tf_op jit(solution)/shard_map/psum | solution.py:98
  127.2 2.8 fusion.80
  130.0 1.9 fusion.42
  132.7 0.3 add_reduce_fusion.96
  133.0 0.3 add_reduce_fusion.95
  133.6 0.3 add_reduce_fusion.89
  134.4 0.3 add_reduce_fusion.88
  135.1 0.3 add_reduce_fusion.87
  135.4 0.3 add_reduce_fusion.86
  136.0 0.2 add_reduce_fusion.85
  137.4 2.0 fusion.40
  140.2 0.3 add_reduce_fusion.68
  140.5 0.3 add_reduce_fusion.67
  141.1 0.3 add_reduce_fusion.61
  141.9 0.3 add_reduce_fusion.60
  142.7 0.3 add_reduce_fusion.59
  142.9 0.3 add_reduce_fusion.58
  143.5 0.2 add_reduce_fusion.57
  145.0 2.0 fusion.38
  147.8 0.3 add_reduce_fusion.40
  148.1 0.3 add_reduce_fusion.39
  148.6 0.3 add_reduce_fusion.33
  149.4 0.3 add_reduce_fusion.32
  150.2 0.3 add_reduce_fusion.31
  150.5 0.3 add_reduce_fusion.30
  151.0 0.2 add_reduce_fusion.29
  152.5 2.2 fusion.36
  155.5 0.3 add_reduce_fusion.12
  155.8 0.3 add_reduce_fusion.11
  156.4 0.3 add_reduce_fusion.5
  157.2 0.3 add_reduce_fusion.4
  157.9 0.3 add_reduce_fusion.3
  158.2 0.3 add_reduce_fusion.2
  158.8 0.2 add_reduce_fusion.1
  160.3 2.0 fusion.34
  162.5 12.4 %convert_multiply_fusion = (f32[16,16,3072]{2,1,0:T(8,128)S(1)}, bf16[16,16,3072]{2,1,0:T(8,128)(2,1)}) fusion(f32[3072]{0:T(1024)S(1)} %copy-done, bf16[16,3072,256]{2,1,0:T(8,128)(2,1)} %param.4, bf16[16,16,256]{2,0,1:T(8,128)(2,1)S(1)} %pad_maximum_fusion), kind=kOutput, calls=%fused_computation.6 | convolution fusion | flops 405012480 | bytes 30027776 | tf_op jit(solution)/shard_map/fkc,fpc->fkp/dot_general | solution.py:102
  175.0 1.5 collective-permute-start
  176.5 34.6 %collective-permute-done = bf16[16,16,3072]{2,1,0:T(8,128)(2,1)S(1)} collective-permute-done((bf16[16,16,3072]{2,1,0:T(8,128)(2,1)}, bf16[16,16,3072]{2,1,0:T(8,128)(2,1)S(1)}, u32[]{:S(2)}, u32[]{:S(2)}) %collective-permute-start) | collective-permute-done | bytes 1572896 | tf_op jit(solution)/shard_map/ppermute | solution.py:17
  211.1 1.5 collective-permute-start.1
  212.6 33.6 %collective-permute-done.1 = bf16[16,16,3072]{2,1,0:T(8,128)(2,1)S(1)} collective-permute-done((bf16[16,16,3072]{2,1,0:T(8,128)(2,1)S(1)}, bf16[16,16,3072]{2,1,0:T(8,128)(2,1)S(1)}, u32[]{:S(2)}, u32[]{:S(2)}) %collective-permute-start.1) | collective-permute-done | bytes 1572896 | tf_op jit(solution)/shard_map/ppermute | solution.py:17
  246.1 1.9 convolution_convert_fusion
  248.1 1.8 fusion.6
  249.9 1.8 fusion.4
  251.7 1.5 fusion.15
  253.2 1.8 fusion.21
  255.0 27.5 %psum.15 = f32[16,2,8,8]{3,2,0,1:T(8,128)S(1)} all-reduce(f32[16,2,8,8]{3,2,0,1:T(8,128)S(1)} %maximum_multiply_fusion.2), channel_id=1, replica_groups=mesh['freq'=4,'space'=8] {'space'}, use_global_device_ids=true, to_apply=%region_258.259 | all-reduce | flops 2048 | bytes 16384 | tf_op jit(solution)/shard_map/psum | solution.py:114
  282.6 0.7 copy.52
  (215 shorter events, 14.6 us)
Async XLA Ops:
  7.2 120.1 %all-reduce.2.cloned.1.call-start = ((), (), s32[]{:S(2)}) async-start(), calls=%async_computation | async-start | bytes 8388608 | tf_op jit(solution)/shard_map/psum | solution.py:98
  158.5 3.9 %copy-start.2 = (s32[16]{0:T(128)S(1)}, s32[16]{0:T(128)}, u32[]{:S(2)}) copy-start(s32[16]{0:T(128)} %param.7) | copy-start | bytes 196
  160.0 2.6 copy-start
  162.4 12.6 %copy-start.1 = (f32[16,8]{0,1:T(8,128)}, f32[16,8]{0,1:T(8,128)S(1)}, u32[]{:S(2)}) copy-start(f32[16,8]{0,1:T(8,128)S(1)} %fusion.33) | copy-start | bytes 1540
  162.5 83.6 %copy-start.3 = (s32[16]{0:T(128)S(1)}, s32[16]{0:T(128)}, u32[]{:S(2)}) copy-start(s32[16]{0:T(128)} %param.6) | copy-start | bytes 196
  175.0 36.1 %collective-permute-start = (bf16[16,16,3072]{2,1,0:T(8,128)(2,1)}, bf16[16,16,3072]{2,1,0:T(8,128)(2,1)S(1)}, u32[]{:S(2)}, u32[]{:S(2)}) collective-permute-start(bf16[16,16,3072]{2,1,0:T(8,128)(2,1)} %get-tuple-element.649), channel_id=1, source_target_pairs={{0,8},{8,0},{16,24},{24,16},{1,9},{9,1},{17,25},{25,17},{2,10},{10... | collective-permute-start | bytes 4718600 | tf_op jit(solution)/shard_map/ppermute | solution.py:17
  211.1 35.0 %collective-permute-start.1 = (bf16[16,16,3072]{2,1,0:T(8,128)(2,1)S(1)}, bf16[16,16,3072]{2,1,0:T(8,128)(2,1)S(1)}, u32[]{:S(2)}, u32[]{:S(2)}) collective-permute-start(bf16[16,16,3072]{2,1,0:T(8,128)(2,1)S(1)} %collective-permute-done), channel_id=1, source_target_pairs={{0,16},{16,0},{8,24},{24,8},{1,17},{17,1},{9,25},{25,9},{2,18},{18... | collective-permute-start | bytes 4718600 | tf_op jit(solution)/shard_map/ppermute | solution.py:17
Sparse Core Ops, SparseCore 0:
  28.0 99.1 all-reduce.1
where the time goes:
time: 290 us
  waiting for transfers between devices  168 us (58%)
  matrix products  51.8 us (18%)
  blocking collectives  27.5 us (9%)
  other arithmetic  24.4 us (8%)
  between operations  14.6 us (5%)
  starting transfers between devices  2.98 us (1%)
    psum x1, waiting for transfers between devices, on_device(): summed = lax.psum(moments, 'space')  99.3 us
    ppermute x2, waiting for transfers between devices, from_partner(): return lax.ppermute(block, axis, route)  68.2 us
    psum x1, blocking collectives, on_device(): coherence = lax.psum(local, 'space')  27.5 us
    dot_general x1, matrix products, on_device(): lax.dot_general(spectra, weighted, (((1,), (1,)), ((0,), (0,))), preferre...  20.7 us
    dot_general x1, matrix products, on_device(): jnp.einsum('fkc,fpc->fkp', coefficient, spectra, preferred_element_type=j...  12.4 us
    reduce_sum x44, other arithmetic, orthonormal(): jnp.sum(early_re * vec_re + early_im * vec_im, axis=1, keepdims=True)  10.6 us
    dot_general x5, matrix products, apply_operator(): jnp.einsum('fkc,fdc->fkd', basis, operator, precision=lax.Precision.HIGHEST)  9.94 us
    dot_general x4, matrix products, inner(): return jnp.einsum('fkp,flp->fkl', left, right, precision=highest)  6.86 us
  transfers between devices with their start and end apart: 3, of which 3 were waited for; matrix products, arithmetic and copies ran while one was open for 0% of the time, Pallas kernels for 0%

commit v1 on v0

--- a/solution.py
+++ b/solution.py
@@ -5,6 +5,11 @@
 
 KMAX = 8
 ITERS = 4
+
+
+def _clear_waves(a0):
+    z_new = jnp.sum(jax.lax.all_gather(a0, axis_name="space"), 0)
+    return z_new
 
 
 def from_partner(block, axis, apart):
@@ -111,7 +116,7 @@
         jnp.bfloat16
     )
     local = cross_terms(modes, chosen, weight, total)
-    coherence = lax.psum(local, "space")
+    coherence = _clear_waves(local)
     return (modes, energy, coherence)
 
 

time: 290 us -> 278 us (0.959)
  blocking collectives: 27.5 us -> 14.9 us
    psum x1 -> x0, blocking collectives: 27.5 us -> none  [on_device(): coherence = lax.psum(local, 'space')]
    all_gather x0 -> x1, blocking collectives: none -> 14.9 us  [_clear_waves(): z_new = jnp.sum(jax.lax.all_gather(a0, axis_name='space'), 0)]
where the time goes in v1:
time: 278 us
  waiting for transfers between devices  168 us (60%)
  matrix products  52 us (19%)
  other arithmetic  25.1 us (9%)
  blocking collectives  14.9 us (5%)
  between operations  14.6 us (5%)
  starting transfers between devices  2.98 us (1%)
    psum x1, waiting for transfers between devices, on_device(): summed = lax.psum(moments, 'space')  99.3 us
    ppermute x2, waiting for transfers between devices, from_partner(): return lax.ppermute(block, axis, route)  68.2 us
    dot_general x1, matrix products, on_device(): lax.dot_general(spectra, weighted, (((1,), (1,)), ((0,), (0,))), preferre...  20.7 us
    all_gather x1, blocking collectives, _clear_waves(): z_new = jnp.sum(jax.lax.all_gather(a0, axis_name='space'), 0)  14.9 us
    dot_general x1, matrix products, on_device(): jnp.einsum('fkc,fpc->fkp', coefficient, spectra, preferred_element_type=j...  12.4 us
    reduce_sum x44, other arithmetic, orthonormal(): jnp.sum(early_re * vec_re + early_im * vec_im, axis=1, keepdims=True)  10.6 us
    dot_general x5, matrix products, apply_operator(): jnp.einsum('fkc,fdc->fkd', basis, operator, precision=lax.Precision.HIGHEST)  9.94 us
    dot_general x4, matrix products, inner(): return jnp.einsum('fkp,flp->fkl', left, right, precision=highest)  7.15 us
  transfers between devices with their start and end apart: 3, of which 3 were waited for; matrix products, arithmetic and copies ran while one was open for 0% of the time, Pallas kernels for 0%

profile of v1, /device:TPU:0, one launch (start us, length us, event | category | flops | bytes accessed | tf_op | source)
XLA Modules:
  0.0 278.1 jit_solution(5551145469311354213)
XLA Ops:
  7.2 20.7 %fusion.2 = f32[16,256,256]{1,2,0:T(8,128)} fusion(bf16[16,3072,256]{2,1,0:T(8,128)(2,1)} %param.4, f32[3072]{0:T(1024)} %param.5), kind=kOutput, calls=%fused_computation.7 | convolution fusion | flops 6480199680 | bytes 29372416 | tf_op jit(solution)/shard_map/dot_general | solution.py:100
  27.9 99.3 %all-reduce.2.cloned.1.call-done = f32[16,256,256]{1,2,0:T(8,128)} async-done(((f32[16,256,256]{1,2,0:T(8,128)}), f32[16,256,256]{1,2,0:T(8,128)}) %all-reduce.2.cloned.1.call-update) | async-done | bytes 4194320 | tf_op jit(solution)/shard_map/psum | solution.py:103
  127.2 2.8 fusion.68
  130.0 1.9 fusion.30
  132.7 0.3 add_reduce_fusion.96
  133.0 0.3 add_reduce_fusion.95
  133.6 0.3 add_reduce_fusion.89
  134.4 0.3 add_reduce_fusion.88
  135.1 0.3 add_reduce_fusion.87
  135.4 0.3 add_reduce_fusion.86
  136.0 0.2 add_reduce_fusion.85
  137.4 2.0 fusion.28
  140.2 0.3 add_reduce_fusion.68
  140.5 0.3 add_reduce_fusion.67
  141.1 0.3 add_reduce_fusion.61
  141.9 0.3 add_reduce_fusion.60
  142.7 0.3 add_reduce_fusion.59
  142.9 0.3 add_reduce_fusion.58
  143.5 0.2 add_reduce_fusion.57
  145.0 2.0 fusion.26
  147.8 0.3 add_reduce_fusion.40
  148.1 0.3 add_reduce_fusion.39
  148.6 0.3 add_reduce_fusion.33
  149.4 0.3 add_reduce_fusion.32
  150.2 0.3 add_reduce_fusion.31
  150.5 0.3 add_reduce_fusion.30
  151.0 0.2 add_reduce_fusion.29
  152.5 2.2 fusion.24
  155.5 0.3 add_reduce_fusion.12
  155.8 0.3 add_reduce_fusion.11
  156.4 0.3 add_reduce_fusion.5
  157.2 0.3 add_reduce_fusion.4
  157.9 0.3 add_reduce_fusion.3
  158.2 0.3 add_reduce_fusion.2
  158.8 0.2 add_reduce_fusion.1
  160.3 2.0 fusion.22
  162.5 12.4 %convert_multiply_fusion = (f32[16,16,3072]{2,1,0:T(8,128)S(1)}, bf16[16,16,3072]{2,1,0:T(8,128)(2,1)}) fusion(f32[3072]{0:T(1024)S(1)} %copy-done, bf16[16,3072,256]{2,1,0:T(8,128)(2,1)} %param.4, bf16[16,16,256]{2,0,1:T(8,128)(2,1)S(1)} %pad_maximum_fusion), kind=kOutput, calls=%fused_computation.6 | convolution fusion | flops 405012480 | bytes 30027776 | tf_op jit(solution)/shard_map/fkc,fpc->fkp/dot_general | solution.py:107
  175.0 1.5 collective-permute-start
  176.5 34.6 %collective-permute-done = bf16[16,16,3072]{2,1,0:T(8,128)(2,1)S(1)} collective-permute-done((bf16[16,16,3072]{2,1,0:T(8,128)(2,1)}, bf16[16,16,3072]{2,1,0:T(8,128)(2,1)S(1)}, u32[]{:S(2)}, u32[]{:S(2)}) %collective-permute-start) | collective-permute-done | bytes 1572896 | tf_op jit(solution)/shard_map/ppermute | solution.py:22
  211.1 1.5 collective-permute-start.1
  212.6 33.6 %collective-permute-done.1 = bf16[16,16,3072]{2,1,0:T(8,128)(2,1)S(1)} collective-permute-done((bf16[16,16,3072]{2,1,0:T(8,128)(2,1)S(1)}, bf16[16,16,3072]{2,1,0:T(8,128)(2,1)S(1)}, u32[]{:S(2)}, u32[]{:S(2)}) %collective-permute-start.1) | collective-permute-done | bytes 1572896 | tf_op jit(solution)/shard_map/ppermute | solution.py:22
  246.1 1.9 convolution_convert_fusion
  248.1 1.8 fusion.10
  249.9 1.8 fusion.4
  251.7 1.8 fusion.6
  253.5 1.8 fusion.8
  255.7 14.9 %all_gather.4 = f32[8,16,2,8,8]{1,4,3,2,0:T(8,128)S(1)} all-gather(f32[1,16,2,8,8]{1,4,3,2,0:T(8,128)S(1)} %maximum_multiply_fusion.2), channel_id=1, replica_groups=mesh['freq'=4,'space'=8] {'space'}, dimensions={0}, use_global_device_ids=true | all-gather | bytes 73728 | tf_op jit(solution)/shard_map/all_gather | solution.py:11
  270.6 0.7 reduce_sum.2579
  (221 shorter events, 15.0 us)
Async XLA Ops:
  7.2 120.1 %all-reduce.2.cloned.1.call-start = ((), (), s32[]{:S(2)}) async-start(), calls=%async_computation | async-start | bytes 8388608 | tf_op jit(solution)/shard_map/psum | solution.py:103
  158.5 3.9 %copy-start.2 = (s32[16]{0:T(128)S(1)}, s32[16]{0:T(128)}, u32[]{:S(2)}) copy-start(s32[16]{0:T(128)} %param.7) | copy-start | bytes 196
  160.0 2.6 copy-start
  162.4 12.6 %copy-start.1 = (f32[16,8]{0,1:T(8,128)}, f32[16,8]{0,1:T(8,128)S(1)}, u32[]{:S(2)}) copy-start(f32[16,8]{0,1:T(8,128)S(1)} %fusion.21) | copy-start | bytes 1540
  162.5 83.6 %copy-start.3 = (s32[16]{0:T(128)S(1)}, s32[16]{0:T(128)}, u32[]{:S(2)}) copy-start(s32[16]{0:T(128)} %param.6) | copy-start | bytes 196
  175.0 36.1 %collective-permute-start = (bf16[16,16,3072]{2,1,0:T(8,128)(2,1)}, bf16[16,16,3072]{2,1,0:T(8,128)(2,1)S(1)}, u32[]{:S(2)}, u32[]{:S(2)}) collective-permute-start(bf16[16,16,3072]{2,1,0:T(8,128)(2,1)} %get-tuple-element.652), channel_id=1, source_target_pairs={{0,8},{8,0},{16,24},{24,16},{1,9},{9,1},{17,25},{25,17},{2,10},{10... | collective-permute-start | bytes 4718600 | tf_op jit(solution)/shard_map/ppermute | solution.py:22
  211.1 35.0 %collective-permute-start.1 = (bf16[16,16,3072]{2,1,0:T(8,128)(2,1)S(1)}, bf16[16,16,3072]{2,1,0:T(8,128)(2,1)S(1)}, u32[]{:S(2)}, u32[]{:S(2)}) collective-permute-start(bf16[16,16,3072]{2,1,0:T(8,128)(2,1)S(1)} %collective-permute-done), channel_id=1, source_target_pairs={{0,16},{16,0},{8,24},{24,8},{1,17},{17,1},{9,25},{25,9},{2,18},{18... | collective-permute-start | bytes 4718600 | tf_op jit(solution)/shard_map/ppermute | solution.py:22
Sparse Core Ops, SparseCore 0:
  28.0 99.1 all-reduce.1
